TPU v7x, 256 devices: a whole 4x4x8 slice. The times are simulated.
256 devices in a mesh: gx: 16 (over z_hi, y), gy: 16 (over z_lo, x, core).
Axes of the slice: x: 4, y: 4, z: 8 (z_hi: 4, z_lo: 2; z = z_hi * 2 + z_lo), core: 2. Of those that a mesh axis runs over, the one named last changes fastest.
Arguments:
- base_scores: float32 [12, 512, 256, 128], P(None, 'gx', 'gy'), may hold values from -6 to 6
- section_scores: float32 [12, 512, 256, 128], P(None, 'gx', 'gy'), may hold values from -6 to 6
- velocity: float32 [3, 512, 256, 128], P(None, 'gx', 'gy'), may hold values from -3 to 3
- diffusivity: float32 [512, 256, 128], P('gx', 'gy'), may hold values from 0.03 to 0.3
- w_first: bfloat16 [256, 12], replicated, may hold values from -1.75 to 1.75
- b_first: float32 [256], replicated, may hold values from -3 to 3
- w_second: bfloat16 [256, 256], replicated, may hold values from -0.375 to 0.375
- b_second: float32 [256], replicated, may hold values from -3 to 3
- w_third: bfloat16 [12, 256], replicated, may hold values from -0.375 to 0.375
- b_third: float32 [12], replicated, may hold values from -3 to 3
- loadings: bfloat16 [12, 300], replicated, may hold values from -0.375 to 0.375
- parcel_species: bfloat16 [8192, 300, 128], P(('gx', 'gy')), may hold values from -6 to 6
- parcel_owner: int32 [8192, 1], P(('gx', 'gy')), may hold values from 0 to 15; in each aligned block of 32 rows (0 to 31, 32 to 63, ...) at most 4 rows name the same one
- parcel_block: int32 [8192], P(('gx', 'gy')), may hold values from 0 to 31
Outputs:
- new_scores: float32 [12, 512, 256, 128], P(None, 'gx', 'gy')
Inputs may be any that keep to these rules, and one draw needn't show every extreme that they name: `parcel_owner`: among the 32 parcel blocks of one device, no tile y index is named by more than 4 of them, and in every draw some device's blocks name one index exactly 4 times.
All inputs are finite; a program needn't handle non-finite values.
Results may differ from a plain program's by a relative error of at most 0.0003.
Values sent between devices are 32-bit elements; how exact they have to be, the bound alone decides.
A program may use at most 64 MiB of HBM per device.

v0:
```python
import math

import jax
import jax.numpy as jnp
from jax import lax
from jax.sharding import PartitionSpec as P

SB = 32


dt_step = 0.25


def padded_2(x, sides, width):
    edges = {}
    for axis, dim in sides:
        size, length = (lax.axis_size(axis), x.shape[dim])
        up = [(i, (i + 1) % size) for i in range(size - 1)]
        last = lax.slice_in_dim(x, length - width, length, axis=dim)
        first = lax.slice_in_dim(x, 0, width, axis=dim)
        edges[dim] = (
            lax.ppermute(last, axis, up),
            lax.ppermute(first, axis, [(b, a) for a, b in up]),
        )
    done = []
    for _, dim in sides:
        low, high = edges[dim]
        around = [(width, width) if d in done else (0, 0) for d in range(x.ndim)]
        x = jnp.concatenate([jnp.pad(low, around), x, jnp.pad(high, around)], axis=dim)
        done.append(dim)
    return x


def regress(block, w_first, b_first, w_second, b_second, w_third, b_third):
    inputs = block.astype(jnp.bfloat16)
    first = jnp.tanh(
        jnp.dot(w_first, inputs, preferred_element_type=jnp.float32) + b_first[:, None]
    ).astype(jnp.bfloat16)
    second = jnp.tanh(
        jnp.dot(w_second, first, preferred_element_type=jnp.float32) + b_second[:, None]
    ).astype(jnp.bfloat16)
    return jnp.dot(w_third, second, preferred_element_type=jnp.float32) + b_third[:, None]


def sources(flat, weights):
    comps, count = flat.shape
    width = math.gcd(count, 4096)
    blocks = flat.reshape(comps, count // width, width).transpose(1, 0, 2)
    result = lax.map(lambda piece: regress(piece, *weights), blocks)
    return result.transpose(1, 0, 2).reshape(comps, count)


def transport_rate(
    center, plus_x, minus_x, plus_y, minus_y, plus_z, minus_z, velocity, diffusivity
):
    drift = (
        velocity[0] * (plus_x - minus_x)
        + velocity[1] * (plus_y - minus_y)
        + velocity[2] * (plus_z - minus_z)
    )
    spread = plus_x + minus_x + plus_y + minus_y + plus_z + minus_z - 6.0 * center
    return diffusivity * spread - 0.5 * drift


def shards(
    base_scores,
    section_scores,
    velocity,
    diffusivity,
    w_first,
    b_first,
    w_second,
    b_second,
    w_third,
    b_third,
    loadings,
    parcel_species,
    parcel_owner,
    parcel_block,
):
    comps, rows_x, rows_y, depth = section_scores.shape
    padded = padded_2(section_scores, (("gx", 1), ("gy", 2)), 1)
    plus_x = padded[:, 2:, 1:-1]
    minus_x = padded[:, :-2, 1:-1]
    plus_y = padded[:, 1:-1, 2:]
    minus_y = padded[:, 1:-1, :-2]
    along_z = jnp.pad(section_scores, ((0, 0), (0, 0), (0, 0), (1, 1)))
    transport = transport_rate(
        section_scores,
        plus_x,
        minus_x,
        plus_y,
        minus_y,
        along_z[..., 2:],
        along_z[..., :-2],
        velocity,
        diffusivity,
    )
    weights = (w_first, b_first, w_second, b_second, w_third, b_third)
    chemistry = sources(section_scores.reshape(comps, -1), weights).reshape(section_scores.shape)
    blocks_here = parcel_species.shape[0]
    block_cells = parcel_species.shape[2]
    projected = jnp.einsum(
        "ks,psc->pkc", loadings, parcel_species, preferred_element_type=jnp.float32
    ).astype(jnp.bfloat16)
    projected = projected.reshape(blocks_here, comps * block_cells)
    owner = parcel_owner[:, 0]
    tiles_y = lax.axis_size("gy")
    capacity = max(2, 2 * blocks_here // tiles_y)
    hits = (owner[:, None] == jnp.arange(tiles_y, dtype=jnp.int32)[None, :]).astype(jnp.int32)
    ranks = jnp.sum(jnp.cumsum(hits, axis=0) * hits, axis=1) - 1
    slot_ids = owner * capacity + ranks
    chosen = slot_ids[None, :] == jnp.arange(tiles_y * capacity, dtype=jnp.int32)[:, None]
    values = jnp.dot(chosen.astype(jnp.bfloat16), projected, preferred_element_type=jnp.float32)
    tags = jnp.sum(jnp.where(chosen, parcel_block[None, :] + 1, 0), axis=1)
    got_values, got_tags = (
        lax.all_to_all(values, "gy", split_axis=0, concat_axis=0, tiled=True),
        lax.all_to_all(tags, "gy", split_axis=0, concat_axis=0, tiled=True),
    )
    placing = (got_tags[None, :] - 1 == jnp.arange(SB, dtype=jnp.int32)[:, None]).astype(
        jnp.float32
    )
    mine = jnp.dot(
        placing, got_values, preferred_element_type=jnp.float32, precision=lax.Precision.HIGHEST
    )
    spray = mine.reshape(SB, comps, block_cells).transpose(1, 0, 2).reshape(comps, SB * block_cells)
    cells = rows_x * rows_y * depth
    spray = jnp.pad(spray, ((0, 0), (0, cells - SB * block_cells))).reshape(section_scores.shape)
    rate = transport + chemistry + spray
    return 0.75 * base_scores + 0.25 * (section_scores + dt_step * rate)


def solution(mesh):
    placed = (
        P(None, "gx", "gy", None),
        P(None, "gx", "gy", None),
        P(None, "gx", "gy", None),
        P("gx", "gy", None),
        P(),
        P(),
        P(),
        P(),
        P(),
        P(),
        P(),
        P(("gx", "gy"), None, None),
        P(("gx", "gy"), None),
        P(("gx", "gy")),
    )
    return jax.shard_map(
        shards, mesh=mesh, in_specs=placed, out_specs=P(None, "gx", "gy", None), check_vma=False
    )
```

profile of v0, /device:TPU:199, one launch (start us, length us, event | category | flops | bytes accessed | tf_op | source)
XLA Modules:
  0.0 171.4 jit_solution(4866745849365181340)
XLA Ops:
  3.1 5.5 %all-to-all-start = ((s32[16,4,1]{1,2,0:T(1,128)}), s32[16,4,1]{1,2,0:T(1,128)S(1)}, u32[]{:S(2)}, u32[]{:S(2)}) async-start(s32[16,4,1]{1,2,0:T(1,128)} %bitcast.9), calls=%async_computation | async-start | bytes 16384 | tf_op jit(solution)/shard_map/all_to_all | solution.py:118
  10.2 3.2 %collective-permute-start.1 = (f32[12,1,16,128]{3,2,1,0:T(8,128)}, f32[12,1,16,128]{3,2,1,0:T(8,128)}, u32[]{:S(2)}, u32[]{:S(2)}) collective-permute-start(f32[12,1,16,128]{3,2,1,0:T(8,128)} %get-tuple-element.101), channel_id=1, source_target_pairs={{0,16},{16,32},{32,48},{48,64},{64,80},{80,96},{96,112},{112,128},... | collective-permute-start | bytes 294920 | tf_op jit(solution)/shard_map/ppermute | solution.py:22
  13.4 5.1 %collective-permute-start = (f32[12,1,16,128]{3,2,1,0:T(8,128)}, f32[12,1,16,128]{3,2,1,0:T(8,128)}, u32[]{:S(2)}, u32[]{:S(2)}) collective-permute-start(f32[12,1,16,128]{3,2,1,0:T(8,128)} %get-tuple-element.100), channel_id=1, source_target_pairs={{16,0},{32,16},{48,32},{64,48},{80,64},{96,80},{112,96},{128,112},... | collective-permute-start | bytes 294920 | tf_op jit(solution)/shard_map/ppermute | solution.py:23
  18.5 2.9 %fusion.27 = (f32[12,32,1,128]{3,2,1,0:T(1,128)}, f32[12,32,1,128]{3,2,1,0:T(1,128)}) fusion(f32[12,32,16,128]{3,2,1,0:T(8,128)} %param.17), kind=kLoop, calls=%fused_computation.53 | loop fusion | bytes 786432 | tf_op jit(solution)/shard_map/slice | solution.py:20
  21.5 3.9 %collective-permute-start.3 = (f32[12,32,1,128]{3,1,2,0:T(8,128)}, f32[12,32,1,128]{3,1,2,0:T(8,128)}, u32[]{:S(2)}, u32[]{:S(2)}) collective-permute-start(f32[12,32,1,128]{3,1,2,0:T(8,128)} %bitcast.18), channel_id=1, source_target_pairs={{0,1},{1,2},{2,3},{3,4},{4,5},{5,6},{6,7},{7,8},{8,9},{9,10},{10,1... | collective-permute-start | bytes 589832 | tf_op jit(solution)/shard_map/ppermute | solution.py:22
  27.4 3.0 %reshape_reshape.6 = bf16[12,16,4096]{2,1,0:T(8,128)(2,1)S(1)} reshape(f32[12,32,16,128]{3,2,1,0:T(8,128)} %param.17) | data formatting | bytes 4718592 | tf_op jit(solution)/shard_map/reshape;reshape | solution.py:48
  30.4 2.5 %fusion.13 = bf16[32,12,128]{2,1,0:T(8,128)(2,1)S(1)} fusion(bf16[32,300,128]{2,0,1:T(8,128)(2,1)} %param.27, bf16[12,300]{1,0:T(8,128)(2,1)S(1)} %copy-done), kind=kOutput, calls=%fused_computation.27 | convolution fusion | flops 29540352 | bytes 2563104 | tf_op jit(solution)/shard_map/ks,psc->pkc/dot_general | solution.py:103
  33.0 96.7 %while.10 = (s32[]{:T(128)}, f32[16,12,4096]{2,1,0:T(8,128)}, bf16[16,12,4096]{2,0,1:T(8,128)(2,1)S(1)}, bf16[256,12]{0,1:T(8,128)(2,1)S(1)}, f32[256]{0:T(256)S...) while((s32[]{:T(128)}, f32[16,12,4096]{2,1,0:T(8,128)}, ...), condition=%wide.region_1.2_spmd, body=%wide.region_0.1_spmd.sunk | while | flops 591446016 | bytes 4896933 | solution.py:49
  33.2 2.1 %fusion.47 = bf16[4096,256]{1,0:T(8,128)(2,1)} fusion(bf16[256,12]{0,1:T(8,128)(2,1)S(1)} %get-tuple-element.185, f32[256]{0:T(256)S(1)} %get-tuple-element.186, bf16[1,12,4096]{2,0,1:T(2,128)(2,1)S(1)} %constant_dynamic-slice_fusion.2), kind=kOutput, calls=%fused_computation.4.clone.1 | convolution fusion | flops 27262976 | bytes 2202624 | tf_op jit(solution)/shard_map/while/body/eval_jaxpr/dot_general | solution.py:37
  35.4 3.7 %fusion.48 = f32[16,12,4096]{2,1,0:T(8,128)} fusion(f32[16,12,4096]{2,1,0:T(8,128)} %get-tuple-element.173, s32[]{:T(128)S(6)} %copy.69, bf16[12,256]{1,0:T(8,128)(2,1)S(1)} %get-tuple-element.189, bf16[4096,256]{1,0:T(8,128)(2,1)} %fusion.47, bf16[256,256]{1,0:T(8,128)(2,1)S(1)} %get-tuple-element.187, f32[256]{0:T(256)S(1)} %get-tuple-element.188, ...), kind=kOutput, calls=%fused_computation.8.clone.1 | convolution fusion | flops 564183040 | bytes 2497588 | tf_op jit(solution)/shard_map/while/body/eval_jaxpr/dot_general | solution.py:42
  39.3 2.1 %fusion.47 = bf16[4096,256]{1,0:T(8,128)(2,1)} fusion(bf16[256,12]{0,1:T(8,128)(2,1)S(1)} %get-tuple-element.185, f32[256]{0:T(256)S(1)} %get-tuple-element.186, bf16[1,12,4096]{2,0,1:T(2,128)(2,1)S(1)} %constant_dynamic-slice_fusion.2), kind=kOutput, calls=%fused_computation.4.clone.1 | convolution fusion | flops 27262976 | bytes 2202624 | tf_op jit(solution)/shard_map/while/body/eval_jaxpr/dot_general | solution.py:37
  41.4 3.7 %fusion.48 = f32[16,12,4096]{2,1,0:T(8,128)} fusion(f32[16,12,4096]{2,1,0:T(8,128)} %get-tuple-element.173, s32[]{:T(128)S(6)} %copy.69, bf16[12,256]{1,0:T(8,128)(2,1)S(1)} %get-tuple-element.189, bf16[4096,256]{1,0:T(8,128)(2,1)} %fusion.47, bf16[256,256]{1,0:T(8,128)(2,1)S(1)} %get-tuple-element.187, f32[256]{0:T(256)S(1)} %get-tuple-element.188, ...), kind=kOutput, calls=%fused_computation.8.clone.1 | convolution fusion | flops 564183040 | bytes 2497588 | tf_op jit(solution)/shard_map/while/body/eval_jaxpr/dot_general | solution.py:42
  47.4 3.7 %fusion.48 = f32[16,12,4096]{2,1,0:T(8,128)} fusion(f32[16,12,4096]{2,1,0:T(8,128)} %get-tuple-element.173, s32[]{:T(128)S(6)} %copy.69, bf16[12,256]{1,0:T(8,128)(2,1)S(1)} %get-tuple-element.189, bf16[4096,256]{1,0:T(8,128)(2,1)} %fusion.47, bf16[256,256]{1,0:T(8,128)(2,1)S(1)} %get-tuple-element.187, f32[256]{0:T(256)S(1)} %get-tuple-element.188, ...), kind=kOutput, calls=%fused_computation.8.clone.1 | convolution fusion | flops 564183040 | bytes 2497588 | tf_op jit(solution)/shard_map/while/body/eval_jaxpr/dot_general | solution.py:42
  53.5 3.7 %fusion.48 = f32[16,12,4096]{2,1,0:T(8,128)} fusion(f32[16,12,4096]{2,1,0:T(8,128)} %get-tuple-element.173, s32[]{:T(128)S(6)} %copy.69, bf16[12,256]{1,0:T(8,128)(2,1)S(1)} %get-tuple-element.189, bf16[4096,256]{1,0:T(8,128)(2,1)} %fusion.47, bf16[256,256]{1,0:T(8,128)(2,1)S(1)} %get-tuple-element.187, f32[256]{0:T(256)S(1)} %get-tuple-element.188, ...), kind=kOutput, calls=%fused_computation.8.clone.1 | convolution fusion | flops 564183040 | bytes 2497588 | tf_op jit(solution)/shard_map/while/body/eval_jaxpr/dot_general | solution.py:42
  59.5 3.7 %fusion.48 = f32[16,12,4096]{2,1,0:T(8,128)} fusion(f32[16,12,4096]{2,1,0:T(8,128)} %get-tuple-element.173, s32[]{:T(128)S(6)} %copy.69, bf16[12,256]{1,0:T(8,128)(2,1)S(1)} %get-tuple-element.189, bf16[4096,256]{1,0:T(8,128)(2,1)} %fusion.47, bf16[256,256]{1,0:T(8,128)(2,1)S(1)} %get-tuple-element.187, f32[256]{0:T(256)S(1)} %get-tuple-element.188, ...), kind=kOutput, calls=%fused_computation.8.clone.1 | convolution fusion | flops 564183040 | bytes 2497588 | tf_op jit(solution)/shard_map/while/body/eval_jaxpr/dot_general | solution.py:42
  65.6 3.7 %fusion.48 = f32[16,12,4096]{2,1,0:T(8,128)} fusion(f32[16,12,4096]{2,1,0:T(8,128)} %get-tuple-element.173, s32[]{:T(128)S(6)} %copy.69, bf16[12,256]{1,0:T(8,128)(2,1)S(1)} %get-tuple-element.189, bf16[4096,256]{1,0:T(8,128)(2,1)} %fusion.47, bf16[256,256]{1,0:T(8,128)(2,1)S(1)} %get-tuple-element.187, f32[256]{0:T(256)S(1)} %get-tuple-element.188, ...), kind=kOutput, calls=%fused_computation.8.clone.1 | convolution fusion | flops 564183040 | bytes 2497588 | tf_op jit(solution)/shard_map/while/body/eval_jaxpr/dot_general | solution.py:42
  71.6 3.7 %fusion.48 = f32[16,12,4096]{2,1,0:T(8,128)} fusion(f32[16,12,4096]{2,1,0:T(8,128)} %get-tuple-element.173, s32[]{:T(128)S(6)} %copy.69, bf16[12,256]{1,0:T(8,128)(2,1)S(1)} %get-tuple-element.189, bf16[4096,256]{1,0:T(8,128)(2,1)} %fusion.47, bf16[256,256]{1,0:T(8,128)(2,1)S(1)} %get-tuple-element.187, f32[256]{0:T(256)S(1)} %get-tuple-element.188, ...), kind=kOutput, calls=%fused_computation.8.clone.1 | convolution fusion | flops 564183040 | bytes 2497588 | tf_op jit(solution)/shard_map/while/body/eval_jaxpr/dot_general | solution.py:42
  77.7 3.7 %fusion.48 = f32[16,12,4096]{2,1,0:T(8,128)} fusion(f32[16,12,4096]{2,1,0:T(8,128)} %get-tuple-element.173, s32[]{:T(128)S(6)} %copy.69, bf16[12,256]{1,0:T(8,128)(2,1)S(1)} %get-tuple-element.189, bf16[4096,256]{1,0:T(8,128)(2,1)} %fusion.47, bf16[256,256]{1,0:T(8,128)(2,1)S(1)} %get-tuple-element.187, f32[256]{0:T(256)S(1)} %get-tuple-element.188, ...), kind=kOutput, calls=%fused_computation.8.clone.1 | convolution fusion | flops 564183040 | bytes 2497588 | tf_op jit(solution)/shard_map/while/body/eval_jaxpr/dot_general | solution.py:42
  83.7 3.7 %fusion.48 = f32[16,12,4096]{2,1,0:T(8,128)} fusion(f32[16,12,4096]{2,1,0:T(8,128)} %get-tuple-element.173, s32[]{:T(128)S(6)} %copy.69, bf16[12,256]{1,0:T(8,128)(2,1)S(1)} %get-tuple-element.189, bf16[4096,256]{1,0:T(8,128)(2,1)} %fusion.47, bf16[256,256]{1,0:T(8,128)(2,1)S(1)} %get-tuple-element.187, f32[256]{0:T(256)S(1)} %get-tuple-element.188, ...), kind=kOutput, calls=%fused_computation.8.clone.1 | convolution fusion | flops 564183040 | bytes 2497588 | tf_op jit(solution)/shard_map/while/body/eval_jaxpr/dot_general | solution.py:42
  87.6 2.1 %fusion.47 = bf16[4096,256]{1,0:T(8,128)(2,1)} fusion(bf16[256,12]{0,1:T(8,128)(2,1)S(1)} %get-tuple-element.185, f32[256]{0:T(256)S(1)} %get-tuple-element.186, bf16[1,12,4096]{2,0,1:T(2,128)(2,1)S(1)} %constant_dynamic-slice_fusion.2), kind=kOutput, calls=%fused_computation.4.clone.1 | convolution fusion | flops 27262976 | bytes 2202624 | tf_op jit(solution)/shard_map/while/body/eval_jaxpr/dot_general | solution.py:37
  89.8 3.7 %fusion.48 = f32[16,12,4096]{2,1,0:T(8,128)} fusion(f32[16,12,4096]{2,1,0:T(8,128)} %get-tuple-element.173, s32[]{:T(128)S(6)} %copy.69, bf16[12,256]{1,0:T(8,128)(2,1)S(1)} %get-tuple-element.189, bf16[4096,256]{1,0:T(8,128)(2,1)} %fusion.47, bf16[256,256]{1,0:T(8,128)(2,1)S(1)} %get-tuple-element.187, f32[256]{0:T(256)S(1)} %get-tuple-element.188, ...), kind=kOutput, calls=%fused_computation.8.clone.1 | convolution fusion | flops 564183040 | bytes 2497588 | tf_op jit(solution)/shard_map/while/body/eval_jaxpr/dot_general | solution.py:42
  95.8 3.7 %fusion.48 = f32[16,12,4096]{2,1,0:T(8,128)} fusion(f32[16,12,4096]{2,1,0:T(8,128)} %get-tuple-element.173, s32[]{:T(128)S(6)} %copy.69, bf16[12,256]{1,0:T(8,128)(2,1)S(1)} %get-tuple-element.189, bf16[4096,256]{1,0:T(8,128)(2,1)} %fusion.47, bf16[256,256]{1,0:T(8,128)(2,1)S(1)} %get-tuple-element.187, f32[256]{0:T(256)S(1)} %get-tuple-element.188, ...), kind=kOutput, calls=%fused_computation.8.clone.1 | convolution fusion | flops 564183040 | bytes 2497588 | tf_op jit(solution)/shard_map/while/body/eval_jaxpr/dot_general | solution.py:42
  101.8 3.7 %fusion.48 = f32[16,12,4096]{2,1,0:T(8,128)} fusion(f32[16,12,4096]{2,1,0:T(8,128)} %get-tuple-element.173, s32[]{:T(128)S(6)} %copy.69, bf16[12,256]{1,0:T(8,128)(2,1)S(1)} %get-tuple-element.189, bf16[4096,256]{1,0:T(8,128)(2,1)} %fusion.47, bf16[256,256]{1,0:T(8,128)(2,1)S(1)} %get-tuple-element.187, f32[256]{0:T(256)S(1)} %get-tuple-element.188, ...), kind=kOutput, calls=%fused_computation.8.clone.1 | convolution fusion | flops 564183040 | bytes 2497588 | tf_op jit(solution)/shard_map/while/body/eval_jaxpr/dot_general | solution.py:42
  105.8 2.1 %fusion.47 = bf16[4096,256]{1,0:T(8,128)(2,1)} fusion(bf16[256,12]{0,1:T(8,128)(2,1)S(1)} %get-tuple-element.185, f32[256]{0:T(256)S(1)} %get-tuple-element.186, bf16[1,12,4096]{2,0,1:T(2,128)(2,1)S(1)} %constant_dynamic-slice_fusion.2), kind=kOutput, calls=%fused_computation.4.clone.1 | convolution fusion | flops 27262976 | bytes 2202624 | tf_op jit(solution)/shard_map/while/body/eval_jaxpr/dot_general | solution.py:37
  107.9 3.7 %fusion.48 = f32[16,12,4096]{2,1,0:T(8,128)} fusion(f32[16,12,4096]{2,1,0:T(8,128)} %get-tuple-element.173, s32[]{:T(128)S(6)} %copy.69, bf16[12,256]{1,0:T(8,128)(2,1)S(1)} %get-tuple-element.189, bf16[4096,256]{1,0:T(8,128)(2,1)} %fusion.47, bf16[256,256]{1,0:T(8,128)(2,1)S(1)} %get-tuple-element.187, f32[256]{0:T(256)S(1)} %get-tuple-element.188, ...), kind=kOutput, calls=%fused_computation.8.clone.1 | convolution fusion | flops 564183040 | bytes 2497588 | tf_op jit(solution)/shard_map/while/body/eval_jaxpr/dot_general | solution.py:42
  113.9 3.7 %fusion.48 = f32[16,12,4096]{2,1,0:T(8,128)} fusion(f32[16,12,4096]{2,1,0:T(8,128)} %get-tuple-element.173, s32[]{:T(128)S(6)} %copy.69, bf16[12,256]{1,0:T(8,128)(2,1)S(1)} %get-tuple-element.189, bf16[4096,256]{1,0:T(8,128)(2,1)} %fusion.47, bf16[256,256]{1,0:T(8,128)(2,1)S(1)} %get-tuple-element.187, f32[256]{0:T(256)S(1)} %get-tuple-element.188, ...), kind=kOutput, calls=%fused_computation.8.clone.1 | convolution fusion | flops 564183040 | bytes 2497588 | tf_op jit(solution)/shard_map/while/body/eval_jaxpr/dot_general | solution.py:42
  120.0 3.7 %fusion.48 = f32[16,12,4096]{2,1,0:T(8,128)} fusion(f32[16,12,4096]{2,1,0:T(8,128)} %get-tuple-element.173, s32[]{:T(128)S(6)} %copy.69, bf16[12,256]{1,0:T(8,128)(2,1)S(1)} %get-tuple-element.189, bf16[4096,256]{1,0:T(8,128)(2,1)} %fusion.47, bf16[256,256]{1,0:T(8,128)(2,1)S(1)} %get-tuple-element.187, f32[256]{0:T(256)S(1)} %get-tuple-element.188, ...), kind=kOutput, calls=%fused_computation.8.clone.1 | convolution fusion | flops 564183040 | bytes 2497588 | tf_op jit(solution)/shard_map/while/body/eval_jaxpr/dot_general | solution.py:42
  126.0 3.7 %fusion.48 = f32[16,12,4096]{2,1,0:T(8,128)} fusion(f32[16,12,4096]{2,1,0:T(8,128)} %get-tuple-element.173, s32[]{:T(128)S(6)} %copy.69, bf16[12,256]{1,0:T(8,128)(2,1)S(1)} %get-tuple-element.189, bf16[4096,256]{1,0:T(8,128)(2,1)} %fusion.47, bf16[256,256]{1,0:T(8,128)(2,1)S(1)} %get-tuple-element.187, f32[256]{0:T(256)S(1)} %get-tuple-element.188, ...), kind=kOutput, calls=%fused_computation.8.clone.1 | convolution fusion | flops 564183040 | bytes 2497588 | tf_op jit(solution)/shard_map/while/body/eval_jaxpr/dot_general | solution.py:42
  131.0 5.7 %copy.37 = f32[12,16,4096]{2,1,0:T(8,128)} copy(f32[12,16,4096]{2,0,1:T(8,128)} %bitcast.71) | data formatting | bytes 6291456 | tf_op jit(solution)/shard_map/transpose | solution.py:50
  136.7 4.7 %reshape_reshape.7 = f32[12,32,16,128]{3,2,1,0:T(8,128)} reshape(f32[12,16,4096]{2,1,0:T(8,128)} %copy.37) | data formatting | bytes 6291456 | tf_op jit(solution)/shard_map/reshape;reshape | solution.py:100
  142.0 6.0 %all-to-all-start.1 = ((f32[16,4,1536]{2,1,0:T(4,128)}), f32[16,4,1536]{2,1,0:T(4,128)S(1)}, u32[]{:S(2)}, u32[]{:S(2)}) async-start(f32[16,4,1536]{2,1,0:T(4,128)} %copy.40), calls=%async_computation.1 | async-start | bytes 786432 | tf_op jit(solution)/shard_map/all_to_all | solution.py:117
  162.9 8.5 %multiply_add_fusion = f32[12,32,16,128]{3,2,1,0:T(8,128)} fusion(f32[12,32,16,128]{3,2,1,0:T(8,128)S(1)} %copy-done.1, f32[12,32,16,128]{3,2,1,0:T(8,128)S(1)} %bitcast.70, f32[12,32,16,128]{3,2,1,0:T(8,128)S(1)} %copy-done.2, f32[12,34,16,128]{3,2,1,0:T(8,128)} %constant_dynamic-update-slice_fusion, f32[12,32,1,128]{3,2,1,0:T(1,128)} %bitcast.19, ...), kind=kLoop, calls=%fused_computation.22 | loop fusion | flops 27525120 | bytes 20709376 | tf_op jit(solution)/shard_map/add | solution.py:130
  (88 shorter events, 52.4 us)
Async XLA Ops:
  0.0 30.4 %copy-start = (bf16[12,300]{1,0:T(8,128)(2,1)S(1)}, bf16[12,300]{1,0:T(8,128)(2,1)}, u32[]{:S(2)}) copy-start(bf16[12,300]{1,0:T(8,128)(2,1)} %param.26) | copy-start | bytes 21604
  3.1 138.3 %all-to-all-start = ((s32[16,4,1]{1,2,0:T(1,128)}), s32[16,4,1]{1,2,0:T(1,128)S(1)}, u32[]{:S(2)}, u32[]{:S(2)}) async-start(s32[16,4,1]{1,2,0:T(1,128)} %bitcast.9), calls=%async_computation | async-start | bytes 16384 | tf_op jit(solution)/shard_map/all_to_all | solution.py:118
  10.2 141.9 %collective-permute-start.1 = (f32[12,1,16,128]{3,2,1,0:T(8,128)}, f32[12,1,16,128]{3,2,1,0:T(8,128)}, u32[]{:S(2)}, u32[]{:S(2)}) collective-permute-start(f32[12,1,16,128]{3,2,1,0:T(8,128)} %get-tuple-element.101), channel_id=1, source_target_pairs={{0,16},{16,32},{32,48},{48,64},{64,80},{80,96},{96,112},{112,128},... | collective-permute-start | bytes 294920 | tf_op jit(solution)/shard_map/ppermute | solution.py:22
  13.4 142.3 %collective-permute-start = (f32[12,1,16,128]{3,2,1,0:T(8,128)}, f32[12,1,16,128]{3,2,1,0:T(8,128)}, u32[]{:S(2)}, u32[]{:S(2)}) collective-permute-start(f32[12,1,16,128]{3,2,1,0:T(8,128)} %get-tuple-element.100), channel_id=1, source_target_pairs={{16,0},{32,16},{48,32},{64,48},{80,64},{96,80},{112,96},{128,112},... | collective-permute-start | bytes 294920 | tf_op jit(solution)/shard_map/ppermute | solution.py:23
  21.5 139.6 %collective-permute-start.3 = (f32[12,32,1,128]{3,1,2,0:T(8,128)}, f32[12,32,1,128]{3,1,2,0:T(8,128)}, u32[]{:S(2)}, u32[]{:S(2)}) collective-permute-start(f32[12,32,1,128]{3,1,2,0:T(8,128)} %bitcast.18), channel_id=1, source_target_pairs={{0,1},{1,2},{2,3},{3,4},{4,5},{5,6},{6,7},{7,8},{8,9},{9,10},{10,1... | collective-permute-start | bytes 589832 | tf_op jit(solution)/shard_map/ppermute | solution.py:22
  25.4 135.7 %collective-permute-start.2 = (f32[12,32,1,128]{3,1,2,0:T(8,128)}, f32[12,32,1,128]{3,1,2,0:T(8,128)}, u32[]{:S(2)}, u32[]{:S(2)}) collective-permute-start(f32[12,32,1,128]{3,1,2,0:T(8,128)} %bitcast.16), channel_id=1, source_target_pairs={{1,0},{2,1},{3,2},{4,3},{5,4},{6,5},{7,6},{8,7},{9,8},{10,9},{11,1... | collective-permute-start | bytes 589832 | tf_op jit(solution)/shard_map/ppermute | solution.py:23
  27.3 5.6 %copy-start.8 = (bf16[256,256]{1,0:T(8,128)(2,1)S(1)}, bf16[256,256]{1,0:T(8,128)(2,1)}, u32[]{:S(2)}) copy-start(bf16[256,256]{1,0:T(8,128)(2,1)} %param.22) | copy-start | bytes 393220
  27.4 5.6 %copy-start.9 = (bf16[256,12]{0,1:T(8,128)(2,1)S(1)}, bf16[256,12]{0,1:T(8,128)(2,1)}, u32[]{:S(2)}) copy-start(bf16[256,12]{0,1:T(8,128)(2,1)} %param.20) | copy-start | bytes 18436
  27.4 5.6 %copy-start.10 = (bf16[12,256]{1,0:T(8,128)(2,1)S(1)}, bf16[12,256]{1,0:T(8,128)(2,1)}, u32[]{:S(2)}) copy-start(bf16[12,256]{1,0:T(8,128)(2,1)} %param.24) | copy-start | bytes 18436
  27.4 5.6 %copy-start.11 = (f32[256]{0:T(256)S(1)}, f32[256]{0:T(256)}, u32[]{:S(2)}) copy-start(f32[256]{0:T(256)} %param.21) | copy-start | bytes 3076
  27.4 5.6 %copy-start.12 = (f32[256]{0:T(256)S(1)}, f32[256]{0:T(256)}, u32[]{:S(2)}) copy-start(f32[256]{0:T(256)} %param.23) | copy-start | bytes 3076
  27.4 5.6 %copy-start.13 = (f32[12]{0:T(128)S(1)}, f32[12]{0:T(128)}, u32[]{:S(2)}) copy-start(f32[12]{0:T(128)} %param.25) | copy-start | bytes 148
  136.7 17.0 %copy-start.1 = (f32[12,32,16,128]{3,2,1,0:T(8,128)S(1)}, f32[12,32,16,128]{3,2,1,0:T(8,128)}, u32[]{:S(2)}) copy-start(f32[12,32,16,128]{3,2,1,0:T(8,128)} %param.17) | copy-start | bytes 9437188
  141.4 0.6 copy-start.7
  142.0 15.4 %all-to-all-start.1 = ((f32[16,4,1536]{2,1,0:T(4,128)}), f32[16,4,1536]{2,1,0:T(4,128)S(1)}, u32[]{:S(2)}, u32[]{:S(2)}) async-start(f32[16,4,1536]{2,1,0:T(4,128)} %copy.40), calls=%async_computation.1 | async-start | bytes 786432 | tf_op jit(solution)/shard_map/all_to_all | solution.py:117
  160.8 1.9 %copy-start.2 = (f32[12,32,16,128]{3,2,1,0:T(8,128)S(1)}, f32[12,32,16,128]{3,2,1,0:T(8,128)}, u32[]{:S(2)}) copy-start(f32[12,32,16,128]{3,2,1,0:T(8,128)} %reshape_reshape.7) | copy-start | bytes 9437188
  160.8 1.9 %copy-start.3 = (f32[32,16,128]{2,1,0:T(8,128)S(1)}, f32[32,16,128]{2,1,0:T(8,128)}, u32[]{:S(2)}) copy-start(f32[32,16,128]{2,1,0:T(8,128)} %get-tuple-element.102) | copy-start | bytes 786436
  160.8 2.0 %copy-start.4 = (f32[32,16,128]{2,1,0:T(8,128)S(1)}, f32[32,16,128]{2,1,0:T(8,128)}, u32[]{:S(2)}) copy-start(f32[32,16,128]{2,1,0:T(8,128)} %get-tuple-element.103) | copy-start | bytes 786436
  160.8 2.0 %copy-start.5 = (f32[32,16,128]{2,1,0:T(8,128)S(1)}, f32[32,16,128]{2,1,0:T(8,128)}, u32[]{:S(2)}) copy-start(f32[32,16,128]{2,1,0:T(8,128)} %get-tuple-element.104) | copy-start | bytes 786436
  160.8 2.1 %copy-start.6 = (f32[32,16,128]{2,1,0:T(8,128)S(1)}, f32[32,16,128]{2,1,0:T(8,128)}, u32[]{:S(2)}) copy-start(f32[32,16,128]{2,1,0:T(8,128)} %param.19) | copy-start | bytes 786436
where the time goes:
time: 174 us; the launch traced here: 171 us
  matrix products  97 us (56%)
  local copies, waits for them, and re-layouts  36.1 us (21%)
  starting transfers between devices  25.6 us (15%)
  other arithmetic  12.2 us (7%)
    dot_general x16, matrix products, regress(): jnp.dot(w_third, second, preferred_element_type=jnp.float32)  59.1 us
    dot_general x16, matrix products, regress(): jnp.dot(w_first, inputs, preferred_element_type=jnp.float32)  34 us
    add x1, other arithmetic, shards(): return 0.75 * base_scores + 0.25 * (section_scores + dt_step * rate)  8.51 us
    unnamed x34, local copies, waits for them, and re-layouts  7.31 us
    ppermute x2, starting transfers between devices, padded_2(): lax.ppermute(last, axis, up)  7.11 us
    ppermute x2, starting transfers between devices, padded_2(): lax.ppermute(first, axis, [(b, a) for a, b in up])  7.01 us
    all_to_all x1, starting transfers between devices, shards(): lax.all_to_all(values, 'gy', split_axis=0, concat_axis=0, tiled=True)  5.99 us
    transpose x1, local copies, waits for them, and re-layouts, sources(): return result.transpose(1, 0, 2).reshape(comps, count)  5.67 us
  transfers between devices with their start and end apart: 6, of which 0 were waited for; matrix products, arithmetic and copies ran while one was open for 76% of the time, Pallas kernels for 0%

commit v1 on v0

v1 whole, which is shorter than its diff:
```python
import jax
import jax.numpy as jnp
from jax import lax
from jax.experimental import pallas as pl
from jax.experimental.pallas import tpu as pltpu
from jax.sharding import PartitionSpec as P

BF = jnp.bfloat16
F32 = jnp.float32
MESH = pl.DeviceIdType.MESH

NPC = 12
SPEC = 300
SPAD = 304
HID = 256
LX, LY, NZ = 32, 16, 128
PB = 32
CAP = 4
SB = 32
NG = 16
CH = 8
NCH = LX // CH
PAIRS = CH // 2
LAG = 2
DT = 0.25
WIDE = (NPC + 1) * NZ
CROWS = 144


def iota(shape, dim):
    return lax.broadcasted_iota(jnp.int32, shape, dim)


def kernel(
    base, section, edges, velocity, diffusivity, w1t, b1, w2, b2, w3, b3, loadings, parcels, owner, block,
    result,
    sec, basev, velv, diffv, outv, chem, par, weave, lrep, lpad, ylo, yhi, send, recv, spr,
    w1tv, b1v, w2v, b2v, w3v, ownv, blkv, loadv, b3s, a16, w1s, b2c, w3p, b3c,
    in_sem, chunk_sem, out_sem, xs, xr, ys, yr, ssem, rsem,
):
    gx = lax.axis_index("gx")
    gy = lax.axis_index("gy")

    barrier = pltpu.get_barrier_semaphore()
    for d in range(1, NG):
        pl.semaphore_signal(barrier, inc=1, device_id={"gy": lax.rem(gy + d, NG)}, device_id_type=MESH)

    @pl.when(gx > 0)
    def _():
        pl.semaphore_signal(barrier, inc=1, device_id={"gx": gx - 1}, device_id_type=MESH)

    @pl.when(gx < NG - 1)
    def _():
        pl.semaphore_signal(barrier, inc=1, device_id={"gx": gx + 1}, device_id_type=MESH)

    small = [
        pltpu.make_async_copy(a, b, in_sem.at[i])
        for i, (a, b) in enumerate(
            [(w1t, w1tv), (b1, b1v), (w2, w2v), (b2, b2v), (w3, w3v), (b3, b3s), (loadings, loadv), (owner, ownv), (block, blkv)]
        )
    ]
    for c in small:
        c.start()

    def chunk_copy(c):
        return pltpu.make_async_copy(
            section.at[:, pl.ds(CH * c, CH)], sec.at[:, pl.ds(1 + CH * c, CH), pl.ds(8, LY)], chunk_sem.at[c]
        )

    for c in (1, 2, 3, 0):
        chunk_copy(c).start()
    big = [
        pltpu.make_async_copy(a, b, in_sem.at[9 + i])
        for i, (a, b) in enumerate([(parcels, par.at[pl.ds(0, SPEC)]), (velocity, velv), (diffusivity, diffv), (base, basev)])
    ]
    for c in big:
        c.start()

    for c in small:
        c.wait()
    par[SPEC:SPAD] = jnp.zeros((SPAD - SPEC, PB, NZ), BF)
    bias = b1v[...]
    hi = bias.astype(BF).astype(F32)
    mid = (bias - hi).astype(BF).astype(F32)
    a16[0:NPC, :] = w1tv[...].astype(F32)
    a16[12:13, :] = hi
    a16[13:14, :] = mid
    a16[14:15, :] = (bias - hi) - mid
    a16[15:16, :] = jnp.zeros((1, HID), F32)
    left = a16[...].T.astype(BF)
    row, lane = iota((16, NZ), 0), iota((16, NZ), 1)
    for j in range(8):
        pick = ((lane < 96) & (lane // 8 == row) & (lane % 8 == j)) | ((lane >= 96) & (lane - 96 + 12 == row) & (row < 15))
        w1s[j] = jnp.dot(left, pick.astype(F32).astype(BF), preferred_element_type=F32).astype(BF)
    b2c[...] = jnp.broadcast_to(b2v[...], (NZ, HID)).T
    w3p[...] = jnp.zeros((16, HID), BF)
    w3p[0:NPC, :] = (w3v[...].astype(F32) * (0.25 * DT)).astype(BF)
    col = jnp.zeros((16, NZ), F32)
    for k in range(NPC):
        col = jnp.where(row == k, b3s[0, k] * (0.25 * DT), col)
    b3c[...] = col
    lpad[...] = jnp.zeros((16, 384), F32)
    lpad[0:NPC, 0:SPEC] = loadv[...].astype(F32)
    for g in range(SPAD // 8):
        tile = lpad[:, (8 * g // 128) * 128 : (8 * g // 128) * 128 + 128]
        lrep[:, 128 * g : 128 * g + 128] = jnp.take_along_axis(tile, (8 * g) % 128 + lane // 16, axis=1)
    diagonal = (iota((16, 256), 1) % 16) == iota((16, 256), 0)

    def weave_one(c, carry):
        for k in range(NPC):
            line = lrep[k : k + 1, pl.ds(pl.multiple_of(256 * c, 256), 256)]
            weave[c, 16 * k : 16 * k + 16, :] = jnp.where(diagonal, jnp.broadcast_to(line, (16, 256)), 0.0).astype(BF)
        return carry

    lax.fori_loop(0, SPAD // 16, weave_one, 0)

    pl.semaphore_wait(barrier, NG - 1 + (gx > 0).astype(jnp.int32) + (gx < NG - 1).astype(jnp.int32))

    def halo_x(up):
        return pltpu.make_async_remote_copy(
            section.at[:, LX - 1 if up else 0], sec.at[:, 0 if up else LX + 1, pl.ds(8, LY)],
            xs.at[0 if up else 1], xr.at[0 if up else 1],
            device_id={"gx": gx + 1 if up else gx - 1}, device_id_type=MESH,
        )

    def halo_y(up):
        return pltpu.make_async_remote_copy(
            edges.at[:, :, LY - 1 if up else 0], ylo if up else yhi,
            ys.at[0 if up else 1], yr.at[0 if up else 1],
            device_id={"gy": gy + 1 if up else gy - 1}, device_id_type=MESH,
        )

    pl.when(gy < NG - 1)(lambda: halo_y(True).start())
    pl.when(gy > 0)(lambda: halo_y(False).start())
    pl.when(gx < NG - 1)(lambda: halo_x(True).start())
    pl.when(gx > 0)(lambda: halo_x(False).start())

    def regress(c, aside):
        n = 8 * PAIRS
        ones = (iota((32, NZ), 0) < 3).astype(F32).astype(BF)
        bias2 = jnp.concatenate([b2c[...]] * 4, axis=1)
        bias3 = jnp.concatenate([b3c[...]] * 4, axis=1)
        cells, first, second = {}, {}, {}
        for t in range(n + 2 * LAG):
            if t < n:
                if t % 8 == 0:
                    parts = []
                    for dx in range(2):
                        for o in range(2):
                            v = sec[:, CH * c + 1 + 2 * (t // 8) + dx, 8 + 8 * o : 16 + 8 * o, :]
                            parts.append(jnp.concatenate([v.reshape(96, NZ).astype(BF), ones], axis=0))
                    cells[t // 8] = jnp.concatenate(parts, axis=1)
                one = jnp.dot(w1s[t % 8], cells[t // 8], preferred_element_type=F32)
            if LAG <= t < n + LAG:
                two = jnp.dot(w2v[...], first.pop(t - LAG), preferred_element_type=F32)
            if t >= 2 * LAG:
                u = t - 2 * LAG
                three = jnp.dot(w3p[...], second.pop(u), preferred_element_type=F32) + bias3
                for dx in range(2):
                    for o in range(2):
                        h = 2 * dx + o
                        chem[CH * c + 2 * (u // 8) + dx, o, pl.ds(u % 8, 16, stride=9), :] = three[:, NZ * h : NZ * h + NZ]
            if t < n:
                first[t] = jnp.tanh(one).astype(BF)
            if LAG <= t < n + LAG:
                second[t - LAG] = jnp.tanh(two + bias2).astype(BF)
            aside(t)

    lane3 = iota((LY, NZ), 1)

    def combine(x, extra=None):
        e = x + 1
        sec[:, e, 7:8, :] = ylo[:, x]
        sec[:, e, 24:25, :] = yhi[:, x]
        d = diffv[x] * (0.25 * DT)
        vx, vy, vz = (velv[i, x] * (-0.125 * DT) for i in range(3))
        up = jnp.where(lane3 == NZ - 1, 0.0, d + vz)
        down = jnp.where(lane3 == 0, 0.0, d - vz)
        c = sec[:, e, 8:24, :]
        total = 0.75 * basev[:, x] + (0.25 - 6.0 * d) * c
        total += (d + vx) * sec[:, e + 1, 8:24, :] + (d - vx) * sec[:, e - 1, 8:24, :]
        total += (d + vy) * sec[:, e, 9:25, :] + (d - vy) * sec[:, e, 7:23, :]
        total += up * pltpu.roll(c, NZ - 1, axis=2) + down * pltpu.roll(c, 1, axis=2)
        if extra is not None:
            total += spr[extra]
        for k in range(NPC):
            for o in range(2):
                outv[k, x, 8 * o : 8 * o + 8, :] = total[k, 8 * o : 8 * o + 8] + chem[x, o, 9 * k : 9 * k + 8, :]

    def out_copy(c):
        return pltpu.make_async_copy(outv.at[:, pl.ds(CH * c, CH)], result.at[:, pl.ds(CH * c, CH)], out_sem.at[c])

    chunk_copy(1).wait()
    regress(1, lambda t: None)

    big[0].wait()
    projected = jnp.zeros((NPC * 16, 2 * NZ), F32)
    for c in range(SPAD // 16):
        right = jnp.concatenate(
            [par[16 * c : 16 * c + 16, 16 * h : 16 * h + 16, :].reshape(256, NZ) for h in range(2)], axis=1
        )
        projected += jnp.dot(weave[c], right, preferred_element_type=F32)
    projected = projected.astype(BF)
    eye = iota((PB, PB), 0) == iota((PB, PB), 1)
    own_row = jnp.broadcast_to(ownv[...].astype(F32), (PB, PB))
    own_col = jnp.sum(jnp.where(eye, own_row, 0.0), axis=1, keepdims=True)
    earlier = (own_row == own_col) & (iota((PB, PB), 0) < iota((PB, PB), 1))
    rank = jnp.sum(jnp.where(earlier, 1.0, 0.0), axis=0, keepdims=True)
    slot = jnp.broadcast_to(ownv[...].astype(F32) * CAP + rank, (NG * CAP, PB))
    chosen = (slot == iota((NG * CAP, PB), 0).astype(F32)).astype(F32).astype(BF)
    blk_row = jnp.broadcast_to(blkv[...].astype(F32) + 1.0, (PB, PB))
    tag = jnp.broadcast_to(jnp.sum(jnp.where(eye, blk_row, 0.0), axis=1, keepdims=True), (PB, NZ)).astype(BF)
    pieces = [
        jnp.concatenate([projected[16 * k : 16 * k + 16, 0:NZ], projected[16 * k : 16 * k + 16, NZ : 2 * NZ]], axis=0)
        for k in range(NPC)
    ]
    values = jnp.dot(chosen, jnp.concatenate(pieces + [tag], axis=1), preferred_element_type=F32)
    for i in range(NG):
        send[i] = values[CAP * i : CAP * i + CAP, :]
    recv[gy] = send[gy]

    def exchange(d):
        peer = lax.rem(gy + d, NG)
        return pltpu.make_async_remote_copy(
            send.at[peer], recv.at[gy], ssem.at[d], rsem.at[d], device_id={"gy": peer}, device_id_type=MESH
        )

    for d in range(1, NG):
        exchange(d).start()

    @pl.when(gx > 0)
    def _():
        halo_x(True).wait_recv()

    @pl.when(gx == 0)
    def _():
        sec[:, 0, 8:24, :] = jnp.zeros((NPC, LY, NZ), F32)

    @pl.when(gx < NG - 1)
    def _():
        halo_x(False).wait_recv()

    @pl.when(gx == NG - 1)
    def _():
        sec[:, LX + 1, 8:24, :] = jnp.zeros((NPC, LY, NZ), F32)

    @pl.when(gy > 0)
    def _():
        halo_y(True).wait_recv()

    @pl.when(gy == 0)
    def _():
        ylo[...] = jnp.zeros((NPC, LX, 1, NZ), F32)

    @pl.when(gy < NG - 1)
    def _():
        halo_y(False).wait_recv()

    @pl.when(gy == NG - 1)
    def _():
        yhi[...] = jnp.zeros((NPC, LX, 1, NZ), F32)

    for c in (2, 3, 0):
        chunk_copy(c).wait()
    for c in big[1:]:
        c.wait()

    def step(b, carry):
        @pl.when(b == NCH - 1)
        def _():
            for d in range(1, NG):
                exchange(d).wait_recv()
            got = jnp.concatenate([recv[i] for i in range(NG)], axis=0)
            place = (got[:, NPC * NZ :] - 1.0 == iota((NG * CAP, NZ), 1).astype(F32)).astype(F32).T[0:SB].astype(BF)
            mine = jnp.dot(place, got[:, 0 : NPC * NZ].astype(BF), preferred_element_type=F32) * (0.25 * DT)
            for k in range(NPC):
                for x in range(2):
                    spr[x, k] = mine[LY * x : LY * x + LY, NZ * k : NZ * k + NZ]

        def aside(t):
            if t % 4 == 2 and t // 4 < CH:
                combine(CH * b + t // 4)

        regress(lax.rem(b + 1, NCH), aside)
        out_copy(b).start()
        return carry

    lax.fori_loop(1, NCH, step, 0)
    for x in range(CH):
        combine(x, x if x < 2 else None)
    out_copy(0).start()
    for d in range(1, NG):
        exchange(d).wait_send()
    pl.when(gy < NG - 1)(lambda: halo_y(True).wait_send())
    pl.when(gy > 0)(lambda: halo_y(False).wait_send())
    pl.when(gx < NG - 1)(lambda: halo_x(True).wait_send())
    pl.when(gx > 0)(lambda: halo_x(False).wait_send())
    for c in range(NCH):
        out_copy(c).wait()


def shards(
    base_scores, section_scores, velocity, diffusivity, w_first, b_first, w_second, b_second, w_third, b_third,
    loadings, parcel_species, parcel_owner, parcel_block,
):
    anywhere = pl.BlockSpec(memory_space=pl.ANY)
    vmem = pltpu.VMEM
    dma = pltpu.SemaphoreType.DMA
    return pl.pallas_call(
        kernel,
        out_shape=jax.ShapeDtypeStruct((NPC, LX, LY, NZ), F32),
        in_specs=[anywhere] * 15,
        out_specs=anywhere,
        scratch_shapes=[
            vmem((NPC, LX + 2, 2 * LY, NZ), F32),
            vmem((NPC, LX, LY, NZ), F32),
            vmem((3, LX, LY, NZ), F32),
            vmem((LX, LY, NZ), F32),
            vmem((NPC, LX, LY, NZ), F32),
            vmem((LX, 2, CROWS, NZ), F32),
            vmem((SPAD, PB, NZ), BF),
            vmem((SPAD // 16, NPC * 16, 256), BF),
            vmem((16, SPAD * 16), F32),
            vmem((16, 384), F32),
            vmem((NPC, LX, 1, NZ), F32),
            vmem((NPC, LX, 1, NZ), F32),
            vmem((NG, CAP, WIDE), F32),
            vmem((NG, CAP, WIDE), F32),
            vmem((2, NPC, LY, NZ), F32),
            vmem((NPC, HID), BF),
            vmem((1, HID), F32),
            vmem((HID, HID), BF),
            vmem((1, HID), F32),
            vmem((NPC, HID), BF),
            vmem((1, PB), jnp.int32),
            vmem((1, PB), jnp.int32),
            vmem((NPC, SPEC), BF),
            pltpu.SMEM((1, NPC), F32),
            vmem((16, HID), F32),
            vmem((8, HID, NZ), BF),
            vmem((HID, NZ), F32),
            vmem((16, HID), BF),
            vmem((16, NZ), F32),
            dma((13,)),
            dma((NCH,)),
            dma((NCH,)),
            dma((2,)),
            dma((2,)),
            dma((2,)),
            dma((2,)),
            dma((NG,)),
            dma((NG,)),
        ],
        compiler_params=pltpu.CompilerParams(collective_id=0, has_side_effects=True),
        name="section_step",
    )(
        base_scores, section_scores, section_scores.reshape(NPC, LX, LY, 1, NZ), velocity, diffusivity,
        w_first.T, b_first.reshape(1, HID), w_second, b_second.reshape(1, HID), w_third, b_third.reshape(1, NPC),
        loadings, parcel_species.transpose(1, 0, 2), parcel_owner.reshape(1, PB), parcel_block.reshape(1, PB),
    )


def solution(mesh):
    placed = (
        P(None, "gx", "gy", None), P(None, "gx", "gy", None), P(None, "gx", "gy", None), P("gx", "gy", None),
        P(), P(), P(), P(), P(), P(), P(),
        P(("gx", "gy"), None, None), P(("gx", "gy"), None), P(("gx", "gy")),
    )
    return jax.shard_map(
        shards, mesh=mesh, in_specs=placed, out_specs=P(None, "gx", "gy", None), check_vma=False
    )
```

time: 174 us -> 40.9 us (0.24)
  the two profiles are of different devices: /device:TPU:199 before, /device:TPU:120 now
where the time goes in v1:
time: 40.9 us; the launch traced here: 40.8 us
  Pallas kernels  37 us (90%)
  local copies, waits for them, and re-layouts  3.76 us (9%)
    pallas_call x1, Pallas kernels, shards(): pl.pallas_call(kernel, out_shape=jax.ShapeDtypeStruct((NPC, LX, LY, NZ),...  37 us
    unnamed x1, local copies, waits for them, and re-layouts  3.76 us

profile of v1, /device:TPU:120, one launch (start us, length us, event | category | flops | bytes accessed | tf_op | source)
XLA Modules:
  0.0 40.8 jit_solution(4431760496692512183)
XLA Ops:
  0.0 37.0 %section_step.1 = f32[12,32,16,128]{3,2,1,0:T(8,128)} custom-call(f32[12,32,16,128]{3,2,1,0:T(8,128)} %base.1, f32[12,32,16,128]{3,2,1,0:T(8,128)} %section.1, f32[12,32,16,1,128]{4,3,2,1,0:T(1,128)} %bitcast.8, f32[3,32,16,128]{3,2,1,0:T(8,128)} %velocity.1, f32[32,16,128]{2,1,0:T(8,128)} %diffusivity.1, bf16[12,256]{1,0:T(8,128)(2,1)} %bitcast.10, ...), custom_call_target="tpu_custom_call" | custom-call | tf_op jit(solution)/shard_map/section_step/pallas_call | solution.py:309
  37.1 3.8 %copy.16 = f32[12,32,16,128]{3,2,1,0:T(8,128)} copy(f32[12,32,16,128]{3,2,1,0:T(8,128)} %section_step.1) | data formatting | bytes 6291456

commit v2 on v1

--- a/solution.py
+++ b/solution.py
@@ -11,14 +11,15 @@
 
 NPC = 12
 SPEC = 300
-SPAD = 304
+SPAD = 320
+PART = 60
 HID = 256
 LX, LY, NZ = 32, 16, 128
 PB = 32
 CAP = 4
 SB = 32
 NG = 16
-CH = 8
+CH = 4
 NCH = LX // CH
 PAIRS = CH // 2
 LAG = 2
@@ -34,9 +35,9 @@
 def kernel(
     base, section, edges, velocity, diffusivity, w1t, b1, w2, b2, w3, b3, loadings, parcels, owner, block,
     result,
-    sec, basev, velv, diffv, outv, chem, par, weave, lrep, lpad, ylo, yhi, send, recv, spr,
+    sec, basev, velv, diffv, chem, par, proj, lrep, lpad, ylo, yhi, send, recv, spr,
     w1tv, b1v, w2v, b2v, w3v, ownv, blkv, loadv, b3s, a16, w1s, b2c, w3p, b3c,
-    in_sem, chunk_sem, out_sem, xs, xr, ys, yr, ssem, rsem,
+    in_sem, par_sem, chunk_sem, xs, xr, ys, yr, ssem, rsem,
 ):
     gx = lax.axis_index("gx")
     gy = lax.axis_index("gy")
@@ -67,11 +68,23 @@
             section.at[:, pl.ds(CH * c, CH)], sec.at[:, pl.ds(1 + CH * c, CH), pl.ds(8, LY)], chunk_sem.at[c]
         )
 
-    for c in (1, 2, 3, 0):
+    def parcel_copy(i):
+        return pltpu.make_async_copy(parcels.at[pl.ds(PART * i, PART)], par.at[pl.ds(PART * i, PART)], par_sem.at[i])
+
+    chunk_copy(1).start()
+    parcel_copy(0).start()
+    parcel_copy(1).start()
+    chunk_copy(2).start()
+    parcel_copy(2).start()
+    chunk_copy(3).start()
+    parcel_copy(3).start()
+    chunk_copy(4).start()
+    parcel_copy(4).start()
+    for c in (5, 6, 7, 0):
         chunk_copy(c).start()
     big = [
         pltpu.make_async_copy(a, b, in_sem.at[9 + i])
-        for i, (a, b) in enumerate([(parcels, par.at[pl.ds(0, SPEC)]), (velocity, velv), (diffusivity, diffv), (base, basev)])
+        for i, (a, b) in enumerate([(velocity, velv), (diffusivity, diffv), (base, basev)])
     ]
     for c in big:
         c.start()
@@ -106,15 +119,7 @@
         lrep[:, 128 * g : 128 * g + 128] = jnp.take_along_axis(tile, (8 * g) % 128 + lane // 16, axis=1)
     diagonal = (iota((16, 256), 1) % 16) == iota((16, 256), 0)
 
-    def weave_one(c, carry):
-        for k in range(NPC):
-            line = lrep[k : k + 1, pl.ds(pl.multiple_of(256 * c, 256), 256)]
-            weave[c, 16 * k : 16 * k + 16, :] = jnp.where(diagonal, jnp.broadcast_to(line, (16, 256)), 0.0).astype(BF)
-        return carry
-
-    lax.fori_loop(0, SPAD // 16, weave_one, 0)
-
-    pl.semaphore_wait(barrier, NG - 1 + (gx > 0).astype(jnp.int32) + (gx < NG - 1).astype(jnp.int32))
+    proj[...] = jnp.zeros((NPC * 16, 2 * NZ), F32)
 
     def halo_x(up):
         return pltpu.make_async_remote_copy(
@@ -129,11 +134,6 @@
             ys.at[0 if up else 1], yr.at[0 if up else 1],
             device_id={"gy": gy + 1 if up else gy - 1}, device_id_type=MESH,
         )
-
-    pl.when(gy < NG - 1)(lambda: halo_y(True).start())
-    pl.when(gy > 0)(lambda: halo_y(False).start())
-    pl.when(gx < NG - 1)(lambda: halo_x(True).start())
-    pl.when(gx > 0)(lambda: halo_x(False).start())
 
     def regress(c, aside):
         n = 8 * PAIRS
@@ -185,22 +185,42 @@
             total += spr[extra]
         for k in range(NPC):
             for o in range(2):
-                outv[k, x, 8 * o : 8 * o + 8, :] = total[k, 8 * o : 8 * o + 8] + chem[x, o, 9 * k : 9 * k + 8, :]
-
-    def out_copy(c):
-        return pltpu.make_async_copy(outv.at[:, pl.ds(CH * c, CH)], result.at[:, pl.ds(CH * c, CH)], out_sem.at[c])
-
-    chunk_copy(1).wait()
-    regress(1, lambda t: None)
-
-    big[0].wait()
-    projected = jnp.zeros((NPC * 16, 2 * NZ), F32)
-    for c in range(SPAD // 16):
-        right = jnp.concatenate(
-            [par[16 * c : 16 * c + 16, 16 * h : 16 * h + 16, :].reshape(256, NZ) for h in range(2)], axis=1
-        )
-        projected += jnp.dot(weave[c], right, preferred_element_type=F32)
-    projected = projected.astype(BF)
+                result[k, x, 8 * o : 8 * o + 8, :] = total[k, 8 * o : 8 * o + 8] + chem[x, o, 9 * k : 9 * k + 8, :]
+
+    def project(c):
+        left = []
+        for k in range(NPC):
+            line = lrep[k : k + 1, pl.ds(pl.multiple_of(256 * c, 256), 256)]
+            left.append(jnp.where(diagonal, jnp.broadcast_to(line, (16, 256)), 0.0).astype(BF))
+        right = [par[pl.ds(16 * c, 16), 16 * h : 16 * h + 16, :].reshape(256, NZ) for h in range(2)]
+        return jnp.dot(jnp.concatenate(left, axis=0), jnp.concatenate(right, axis=1), preferred_element_type=F32)
+
+    def open_step(b, carry):
+        chunk_copy(b + 1).wait()
+        parcel_copy(b + 1).wait()
+        got = []
+
+        def aside(t):
+            if t % 3 == 2 and len(got) < 5:
+                got.append(project(5 * b + len(got)))
+
+        regress(b + 1, aside)
+        proj[...] += sum(got)
+        return carry
+
+    parcel_copy(0).wait()
+    lax.fori_loop(0, 1, open_step, 0)
+
+    pl.semaphore_wait(barrier, NG - 1 + (gx > 0).astype(jnp.int32) + (gx < NG - 1).astype(jnp.int32))
+
+    pl.when(gy < NG - 1)(lambda: halo_y(True).start())
+    pl.when(gy > 0)(lambda: halo_y(False).start())
+    pl.when(gx < NG - 1)(lambda: halo_x(True).start())
+    pl.when(gx > 0)(lambda: halo_x(False).start())
+
+    lax.fori_loop(1, NCH // 2, open_step, 0)
+
+    projected = proj[...].astype(BF)
     eye = iota((PB, PB), 0) == iota((PB, PB), 1)
     own_row = jnp.broadcast_to(ownv[...].astype(F32), (PB, PB))
     own_col = jnp.sum(jnp.where(eye, own_row, 0.0), axis=1, keepdims=True)
@@ -260,9 +280,9 @@
     def _():
         yhi[...] = jnp.zeros((NPC, LX, 1, NZ), F32)
 
-    for c in (2, 3, 0):
+    for c in (5, 6, 7, 0):
         chunk_copy(c).wait()
-    for c in big[1:]:
+    for c in big:
         c.wait()
 
     def step(b, carry):
@@ -277,49 +297,48 @@
                 for x in range(2):
                     spr[x, k] = mine[LY * x : LY * x + LY, NZ * k : NZ * k + NZ]
 
+        late, early = 2 * b - NCH + 1, jnp.maximum(2 * b - NCH, 1)
+
         def aside(t):
-            if t % 4 == 2 and t // 4 < CH:
-                combine(CH * b + t // 4)
-
-        regress(lax.rem(b + 1, NCH), aside)
-        out_copy(b).start()
+            if t % 2 == 1 and t // 2 < 2 * CH:
+                i = t // 2
+                combine(CH * (early if i < CH else late) + i % CH)
+
+        chunk = lax.rem(b + 1, NCH)
+        regress(chunk, aside)
         return carry
 
-    lax.fori_loop(1, NCH, step, 0)
+    lax.fori_loop(NCH // 2, NCH, step, 0)
     for x in range(CH):
         combine(x, x if x < 2 else None)
-    out_copy(0).start()
     for d in range(1, NG):
         exchange(d).wait_send()
     pl.when(gy < NG - 1)(lambda: halo_y(True).wait_send())
     pl.when(gy > 0)(lambda: halo_y(False).wait_send())
     pl.when(gx < NG - 1)(lambda: halo_x(True).wait_send())
     pl.when(gx > 0)(lambda: halo_x(False).wait_send())
-    for c in range(NCH):
-        out_copy(c).wait()
 
 
 def shards(
     base_scores, section_scores, velocity, diffusivity, w_first, b_first, w_second, b_second, w_third, b_third,
     loadings, parcel_species, parcel_owner, parcel_block,
 ):
-    anywhere = pl.BlockSpec(memory_space=pl.ANY)
+    anywhere = pl.BlockSpec(memory_space=pltpu.HBM)
     vmem = pltpu.VMEM
     dma = pltpu.SemaphoreType.DMA
     return pl.pallas_call(
         kernel,
         out_shape=jax.ShapeDtypeStruct((NPC, LX, LY, NZ), F32),
         in_specs=[anywhere] * 15,
-        out_specs=anywhere,
+        out_specs=pl.BlockSpec(memory_space=pltpu.VMEM),
         scratch_shapes=[
             vmem((NPC, LX + 2, 2 * LY, NZ), F32),
             vmem((NPC, LX, LY, NZ), F32),
             vmem((3, LX, LY, NZ), F32),
             vmem((LX, LY, NZ), F32),
-            vmem((NPC, LX, LY, NZ), F32),
             vmem((LX, 2, CROWS, NZ), F32),
             vmem((SPAD, PB, NZ), BF),
-            vmem((SPAD // 16, NPC * 16, 256), BF),
+            vmem((NPC * 16, 2 * NZ), F32),
             vmem((16, SPAD * 16), F32),
             vmem((16, 384), F32),
             vmem((NPC, LX, 1, NZ), F32),
@@ -341,8 +360,8 @@
             vmem((HID, NZ), F32),
             vmem((16, HID), BF),
             vmem((16, NZ), F32),
-            dma((13,)),
-            dma((NCH,)),
+            dma((12,)),
+            dma((SPEC // PART,)),
             dma((NCH,)),
             dma((2,)),
             dma((2,)),
@@ -351,13 +370,13 @@
             dma((NG,)),
             dma((NG,)),
         ],
-        compiler_params=pltpu.CompilerParams(collective_id=0, has_side_effects=True),
+        compiler_params=pltpu.CompilerParams(collective_id=0, has_side_effects=True, vmem_limit_bytes=40 * 1024 * 1024),
         name="section_step",
-    )(
+    )(*[pltpu.with_memory_space_constraint(v, pltpu.HBM) for v in (
         base_scores, section_scores, section_scores.reshape(NPC, LX, LY, 1, NZ), velocity, diffusivity,
         w_first.T, b_first.reshape(1, HID), w_second, b_second.reshape(1, HID), w_third, b_third.reshape(1, NPC),
         loadings, parcel_species.transpose(1, 0, 2), parcel_owner.reshape(1, PB), parcel_block.reshape(1, PB),
-    )
+    )])
 
 
 def solution(mesh):

time: 40.9 us -> 33.7 us (0.82)
  the two profiles are of different devices: /device:TPU:120 before, /device:TPU:199 now
where the time goes in v2:
time: 33.7 us; the launch traced here: 33.5 us
  Pallas kernels  31.9 us (95%)
  local copies, waits for them, and re-layouts  1.67 us (5%)
    pallas_call x1, Pallas kernels, shards(): pl.pallas_call(kernel, out_shape=jax.ShapeDtypeStruct((NPC, LX, LY, NZ),...  31.9 us
    unnamed x1, local copies, waits for them, and re-layouts  1.67 us

profile of v2, /device:TPU:199, one launch (start us, length us, event | category | flops | bytes accessed | tf_op | source)
XLA Modules:
  0.0 33.5 jit_solution(12439844297488120140)
XLA Ops:
  0.0 31.9 %section_step.1 = f32[12,32,16,128]{3,2,1,0:T(8,128)S(1)} custom-call(f32[12,32,16,128]{3,2,1,0:T(8,128)} %base.1, f32[12,32,16,128]{3,2,1,0:T(8,128)} %section.1, f32[12,32,16,1,128]{4,3,2,1,0:T(1,128)} %bitcast.8, f32[3,32,16,128]{3,2,1,0:T(8,128)} %velocity.1, f32[32,16,128]{2,1,0:T(8,128)} %diffusivity.1, bf16[12,256]{1,0:T(8,128)(2,1)} %bitcast.10, ...), custom_call_target="tpu_custom_call" | custom-call | tf_op jit(solution)/shard_map/section_step/pallas_call | solution.py:329
  31.9 1.7 %copy.16 = f32[12,32,16,128]{3,2,1,0:T(8,128)} copy(f32[12,32,16,128]{3,2,1,0:T(8,128)S(1)} %section_step.1) | data formatting | bytes 6291456

commit v3 on v2

--- a/solution.py
+++ b/solution.py
@@ -22,7 +22,6 @@
 CH = 4
 NCH = LX // CH
 PAIRS = CH // 2
-LAG = 2
 DT = 0.25
 WIDE = (NPC + 1) * NZ
 CROWS = 144
@@ -141,7 +140,14 @@
         bias2 = jnp.concatenate([b2c[...]] * 4, axis=1)
         bias3 = jnp.concatenate([b3c[...]] * 4, axis=1)
         cells, first, second = {}, {}, {}
-        for t in range(n + 2 * LAG):
+        for t in range(n + 3):
+            if t >= 3:
+                u = t - 3
+                three = jnp.dot(w3p[...], second.pop(u), preferred_element_type=F32) + bias3
+                for dx in range(2):
+                    for o in range(2):
+                        h = 2 * dx + o
+                        chem[CH * c + 2 * (u // 8) + dx, o, pl.ds(u % 8, 16, stride=9), :] = three[:, NZ * h : NZ * h + NZ]
             if t < n:
                 if t % 8 == 0:
                     parts = []
@@ -151,19 +157,10 @@
                             parts.append(jnp.concatenate([v.reshape(96, NZ).astype(BF), ones], axis=0))
                     cells[t // 8] = jnp.concatenate(parts, axis=1)
                 one = jnp.dot(w1s[t % 8], cells[t // 8], preferred_element_type=F32)
-            if LAG <= t < n + LAG:
-                two = jnp.dot(w2v[...], first.pop(t - LAG), preferred_element_type=F32)
-            if t >= 2 * LAG:
-                u = t - 2 * LAG
-                three = jnp.dot(w3p[...], second.pop(u), preferred_element_type=F32) + bias3
-                for dx in range(2):
-                    for o in range(2):
-                        h = 2 * dx + o
-                        chem[CH * c + 2 * (u // 8) + dx, o, pl.ds(u % 8, 16, stride=9), :] = three[:, NZ * h : NZ * h + NZ]
-            if t < n:
                 first[t] = jnp.tanh(one).astype(BF)
-            if LAG <= t < n + LAG:
-                second[t - LAG] = jnp.tanh(two + bias2).astype(BF)
+            if 1 <= t <= n:
+                two = jnp.dot(w2v[...], first.pop(t - 1), preferred_element_type=F32)
+                second[t - 1] = jnp.tanh(two + bias2).astype(BF)
             aside(t)
 
     lane3 = iota((LY, NZ), 1)

time: 33.7 us -> 31 us (0.920)
  Pallas kernels: 31.9 us -> 29.2 us
    pallas_call x1, Pallas kernels: 31.9 us -> 29.2 us  [shards(): pl.pallas_call(kernel, out_shape=jax.ShapeDtypeStruct((NPC, LX, LY, NZ),...]
where the time goes in v3:
time: 31 us; the launch traced here: 30.9 us
  Pallas kernels  29.2 us (94%)
  local copies, waits for them, and re-layouts  1.67 us (5%)
    pallas_call x1, Pallas kernels, shards(): pl.pallas_call(kernel, out_shape=jax.ShapeDtypeStruct((NPC, LX, LY, NZ),...  29.2 us
    unnamed x1, local copies, waits for them, and re-layouts  1.67 us

profile of v3, /device:TPU:199, one launch (start us, length us, event | category | flops | bytes accessed | tf_op | source)
XLA Modules:
  0.0 30.9 jit_solution(1949783487030864663)
XLA Ops:
  0.0 29.2 %section_step.1 = f32[12,32,16,128]{3,2,1,0:T(8,128)S(1)} custom-call(f32[12,32,16,128]{3,2,1,0:T(8,128)} %base.1, f32[12,32,16,128]{3,2,1,0:T(8,128)} %section.1, f32[12,32,16,1,128]{4,3,2,1,0:T(1,128)} %bitcast.8, f32[3,32,16,128]{3,2,1,0:T(8,128)} %velocity.1, f32[32,16,128]{2,1,0:T(8,128)} %diffusivity.1, bf16[12,256]{1,0:T(8,128)(2,1)} %bitcast.10, ...), custom_call_target="tpu_custom_call" | custom-call | tf_op jit(solution)/shard_map/section_step/pallas_call | solution.py:326
  29.2 1.7 %copy.16 = f32[12,32,16,128]{3,2,1,0:T(8,128)} copy(f32[12,32,16,128]{3,2,1,0:T(8,128)S(1)} %section_step.1) | data formatting | bytes 6291456

commit v4 on v3

--- a/solution.py
+++ b/solution.py
@@ -35,7 +35,7 @@
     base, section, edges, velocity, diffusivity, w1t, b1, w2, b2, w3, b3, loadings, parcels, owner, block,
     result,
     sec, basev, velv, diffv, chem, par, proj, lrep, lpad, ylo, yhi, send, recv, spr,
-    w1tv, b1v, w2v, b2v, w3v, ownv, blkv, loadv, b3s, a16, w1s, b2c, w3p, b3c,
+    w1tv, b1v, w2v, b2v, w3v, ownv, blkv, loadv, b3s, a16, w1s, b2c, w3p, b3c, rest,
     in_sem, par_sem, chunk_sem, xs, xr, ys, yr, ssem, rsem,
 ):
     gx = lax.axis_index("gx")
@@ -105,7 +105,7 @@
         pick = ((lane < 96) & (lane // 8 == row) & (lane % 8 == j)) | ((lane >= 96) & (lane - 96 + 12 == row) & (row < 15))
         w1s[j] = jnp.dot(left, pick.astype(F32).astype(BF), preferred_element_type=F32).astype(BF)
     b2c[...] = jnp.broadcast_to(b2v[...], (NZ, HID)).T
-    w3p[...] = jnp.zeros((16, HID), BF)
+    w3p[...] = jnp.zeros((64, HID), BF)
     w3p[0:NPC, :] = (w3v[...].astype(F32) * (0.25 * DT)).astype(BF)
     col = jnp.zeros((16, NZ), F32)
     for k in range(NPC):
@@ -143,7 +143,9 @@
         for t in range(n + 3):
             if t >= 3:
                 u = t - 3
-                three = jnp.dot(w3p[...], second.pop(u), preferred_element_type=F32) + bias3
+                three = jnp.dot(w3p[...], second.pop(u), preferred_element_type=F32)
+                rest[...] = three[16:, :]
+                three = three[:16, :] + bias3
                 for dx in range(2):
                     for o in range(2):
                         h = 2 * dx + o
@@ -190,7 +192,10 @@
             line = lrep[k : k + 1, pl.ds(pl.multiple_of(256 * c, 256), 256)]
             left.append(jnp.where(diagonal, jnp.broadcast_to(line, (16, 256)), 0.0).astype(BF))
         right = [par[pl.ds(16 * c, 16), 16 * h : 16 * h + 16, :].reshape(256, NZ) for h in range(2)]
-        return jnp.dot(jnp.concatenate(left, axis=0), jnp.concatenate(right, axis=1), preferred_element_type=F32)
+        right = jnp.concatenate(right, axis=1)
+        return jnp.concatenate(
+            [jnp.dot(jnp.concatenate(left[i : i + 6], axis=0), right, preferred_element_type=F32) for i in (0, 6)], axis=0
+        )
 
     def open_step(b, carry):
         chunk_copy(b + 1).wait()
@@ -198,8 +203,9 @@
         got = []
 
         def aside(t):
-            if t % 3 == 2 and len(got) < 5:
-                got.append(project(5 * b + len(got)))
+            if t == 1:
+                for _ in range(5):
+                    got.append(project(5 * b + len(got)))
 
         regress(b + 1, aside)
         proj[...] += sum(got)
@@ -283,17 +289,6 @@
         c.wait()
 
     def step(b, carry):
-        @pl.when(b == NCH - 1)
-        def _():
-            for d in range(1, NG):
-                exchange(d).wait_recv()
-            got = jnp.concatenate([recv[i] for i in range(NG)], axis=0)
-            place = (got[:, NPC * NZ :] - 1.0 == iota((NG * CAP, NZ), 1).astype(F32)).astype(F32).T[0:SB].astype(BF)
-            mine = jnp.dot(place, got[:, 0 : NPC * NZ].astype(BF), preferred_element_type=F32) * (0.25 * DT)
-            for k in range(NPC):
-                for x in range(2):
-                    spr[x, k] = mine[LY * x : LY * x + LY, NZ * k : NZ * k + NZ]
-
         late, early = 2 * b - NCH + 1, jnp.maximum(2 * b - NCH, 1)
 
         def aside(t):
@@ -306,6 +301,14 @@
         return carry
 
     lax.fori_loop(NCH // 2, NCH, step, 0)
+    for d in range(1, NG):
+        exchange(d).wait_recv()
+    got = jnp.concatenate([recv[i] for i in range(NG)], axis=0)
+    place = (got[:, NPC * NZ :] - 1.0 == iota((NG * CAP, NZ), 1).astype(F32)).astype(F32).T[0:SB].astype(BF)
+    mine = jnp.dot(place, got[:, 0 : NPC * NZ].astype(BF), preferred_element_type=F32) * (0.25 * DT)
+    for k in range(NPC):
+        for x in range(2):
+            spr[x, k] = mine[LY * x : LY * x + LY, NZ * k : NZ * k + NZ]
     for x in range(CH):
         combine(x, x if x < 2 else None)
     for d in range(1, NG):
@@ -355,8 +358,9 @@
             vmem((16, HID), F32),
             vmem((8, HID, NZ), BF),
             vmem((HID, NZ), F32),
-            vmem((16, HID), BF),
+            vmem((64, HID), BF),
             vmem((16, NZ), F32),
+            vmem((48, 4 * NZ), F32),
             dma((12,)),
             dma((SPEC // PART,)),
             dma((NCH,)),

time: 31 us -> 30.4 us (0.981)
  Pallas kernels: 29.2 us -> 28.6 us
    pallas_call x1, Pallas kernels: 29.2 us -> 28.6 us  [shards(): pl.pallas_call(kernel, out_shape=jax.ShapeDtypeStruct((NPC, LX, LY, NZ),...]
where the time goes in v4:
time: 30.4 us; the launch traced here: 30.3 us
  Pallas kernels  28.6 us (94%)
  local copies, waits for them, and re-layouts  1.67 us (5%)
    pallas_call x1, Pallas kernels, shards(): pl.pallas_call(kernel, out_shape=jax.ShapeDtypeStruct((NPC, LX, LY, NZ),...  28.6 us
    unnamed x1, local copies, waits for them, and re-layouts  1.67 us

profile of v4, /device:TPU:199, one launch (start us, length us, event | category | flops | bytes accessed | tf_op | source)
XLA Modules:
  0.0 30.3 jit_solution(12576265358979870810)
XLA Ops:
  0.0 28.6 %section_step.1 = f32[12,32,16,128]{3,2,1,0:T(8,128)S(1)} custom-call(f32[12,32,16,128]{3,2,1,0:T(8,128)} %base.1, f32[12,32,16,128]{3,2,1,0:T(8,128)} %section.1, f32[12,32,16,1,128]{4,3,2,1,0:T(1,128)} %bitcast.8, f32[3,32,16,128]{3,2,1,0:T(8,128)} %velocity.1, f32[32,16,128]{2,1,0:T(8,128)} %diffusivity.1, bf16[12,256]{1,0:T(8,128)(2,1)} %bitcast.10, ...), custom_call_target="tpu_custom_call" | custom-call | tf_op jit(solution)/shard_map/section_step/pallas_call | solution.py:329
  28.6 1.7 %copy.16 = f32[12,32,16,128]{3,2,1,0:T(8,128)} copy(f32[12,32,16,128]{3,2,1,0:T(8,128)S(1)} %section_step.1) | data formatting | bytes 6291456

commit v5 on v4

--- a/solution.py
+++ b/solution.py
@@ -105,7 +105,7 @@
         pick = ((lane < 96) & (lane // 8 == row) & (lane % 8 == j)) | ((lane >= 96) & (lane - 96 + 12 == row) & (row < 15))
         w1s[j] = jnp.dot(left, pick.astype(F32).astype(BF), preferred_element_type=F32).astype(BF)
     b2c[...] = jnp.broadcast_to(b2v[...], (NZ, HID)).T
-    w3p[...] = jnp.zeros((64, HID), BF)
+    w3p[...] = jnp.zeros((48, HID), BF)
     w3p[0:NPC, :] = (w3v[...].astype(F32) * (0.25 * DT)).astype(BF)
     col = jnp.zeros((16, NZ), F32)
     for k in range(NPC):
@@ -358,9 +358,9 @@
             vmem((16, HID), F32),
             vmem((8, HID, NZ), BF),
             vmem((HID, NZ), F32),
-            vmem((64, HID), BF),
+            vmem((48, HID), BF),
             vmem((16, NZ), F32),
-            vmem((48, 4 * NZ), F32),
+            vmem((32, 4 * NZ), F32),
             dma((12,)),
             dma((SPEC // PART,)),
             dma((NCH,)),

time: 30.4 us -> 30 us (0.987)
  Pallas kernels: 28.6 us -> 28.2 us
    pallas_call x1, Pallas kernels: 28.6 us -> 28.2 us  [shards(): pl.pallas_call(kernel, out_shape=jax.ShapeDtypeStruct((NPC, LX, LY, NZ),...]
where the time goes in v5:
time: 30 us; the launch traced here: 29.9 us
  Pallas kernels  28.2 us (94%)
  local copies, waits for them, and re-layouts  1.67 us (6%)
    pallas_call x1, Pallas kernels, shards(): pl.pallas_call(kernel, out_shape=jax.ShapeDtypeStruct((NPC, LX, LY, NZ),...  28.2 us
    unnamed x1, local copies, waits for them, and re-layouts  1.67 us

profile of v5, /device:TPU:199, one launch (start us, length us, event | category | flops | bytes accessed | tf_op | source)
XLA Modules:
  0.0 29.9 jit_solution(14382539853849998438)
XLA Ops:
  0.0 28.2 %section_step.1 = f32[12,32,16,128]{3,2,1,0:T(8,128)S(1)} custom-call(f32[12,32,16,128]{3,2,1,0:T(8,128)} %base.1, f32[12,32,16,128]{3,2,1,0:T(8,128)} %section.1, f32[12,32,16,1,128]{4,3,2,1,0:T(1,128)} %bitcast.8, f32[3,32,16,128]{3,2,1,0:T(8,128)} %velocity.1, f32[32,16,128]{2,1,0:T(8,128)} %diffusivity.1, bf16[12,256]{1,0:T(8,128)(2,1)} %bitcast.10, ...), custom_call_target="tpu_custom_call" | custom-call | tf_op jit(solution)/shard_map/section_step/pallas_call | solution.py:329
  28.2 1.7 %copy.16 = f32[12,32,16,128]{3,2,1,0:T(8,128)} copy(f32[12,32,16,128]{3,2,1,0:T(8,128)S(1)} %section_step.1) | data formatting | bytes 6291456
